TPU v7x, 32 devices: a whole 2x2x4 slice. The times are simulated.
32 devices in a mesh: ctx: 16 (over z, x, core), head: 2 (over y).
Axes of the slice: x: 2, y: 2, z: 4, core: 2. Of those that a mesh axis runs over, the one named last changes fastest.
Arguments:
- queries: bfloat16 [8192, 16, 128], P('ctx', 'head'), may hold values from -160 to 160, as said below
- keys: bfloat16 [8192, 2, 128], P('ctx', 'head'), may hold values from -4 to 4
- values: bfloat16 [8192, 2, 128], P('ctx', 'head'), may hold values from -6 to 6
- doc_lengths: int32 [32], replicated, may hold values from 1 to 4096, 8192 in all
Outputs:
- attended: bfloat16 [8192, 2048], P(('ctx', 'head'))
Inputs may be any that keep to these rules, and one draw needn't show every extreme that they name: `queries`: queries of several heads for a few tokens may be large multiples of sums of earlier keys of the same key head. `doc_lengths`: the lengths sum to 8192; the largest is exactly 4096.
All inputs are finite; a program needn't handle non-finite values.
Results may differ from a plain program's by a relative error of at most 0.0033.
Values may be sent and summed in bfloat16 or wider, within the bound.
A program may use at most 64 MiB of HBM per device.

v0:
```python
import functools
import math

import jax
import jax.numpy as jnp
from jax import lax
from jax.experimental import pallas as pl
from jax.experimental.pallas import tpu as pltpu
from jax.sharding import PartitionSpec as P

MESH = pl.DeviceIdType.MESH
BIG = 1e30
TILE = 512


def kernel(n, heads, lens_ref, q_ref, k_ref, v_ref, out_ref,
           kbuf, vbuf, kdoc, qaug, acc, top, norm, stage,
           send_sem, recv_sem, osend_sem, orecv_sem):
    rows, hdim = k_ref.shape
    total_rows = q_ref.shape[0]
    group = total_rows // rows
    me = lax.axis_index("ctx")
    mine = lax.axis_index("head")
    pos = me % 4
    core = pos % 2
    col = pos // 2
    mate = me + 1 - 2 * core
    across = me + 2 - 4 * col
    pos_m = pos + 1 - 2 * core
    pos_x = pos + 2 - 4 * col
    pos_d = pos_x + pos_m - pos
    has1 = me >= 4
    has2 = me >= 8
    feeds = me + 4 < n
    right = col == 1
    leftc = col == 0

    barrier = pltpu.get_barrier_semaphore()
    for peer in (mate, across):
        pl.semaphore_signal(barrier, inc=1, device_id={"ctx": peer}, device_id_type=MESH)

    @pl.when(has1)
    def _():
        pl.semaphore_signal(barrier, inc=1, device_id={"ctx": me - 4}, device_id_type=MESH)

    @pl.when(feeds)
    def _():
        pl.semaphore_signal(barrier, inc=1, device_id={"ctx": me + 4}, device_id_type=MESH)

    for d in range(1, heads):
        pl.semaphore_signal(barrier, inc=1, device_id={"head": (mine + d) % heads}, device_id_type=MESH)
    pl.semaphore_wait(barrier, 1 + heads + has1.astype(jnp.int32) + feeds.astype(jnp.int32))

    def copies(lane, slot, to_slot, target):
        made = []
        for w, buf, own in ((0, kbuf, k_ref), (1, vbuf, v_ref)):
            made.append(pltpu.make_async_remote_copy(
                src_ref=own if slot is None else buf.at[slot],
                dst_ref=buf.at[to_slot],
                send_sem=send_sem.at[lane, w],
                recv_sem=recv_sem.at[to_slot, w],
                device_id={"ctx": target},
                device_id_type=MESH,
            ))
        return made

    moves = {
        "D0": (copies(0, None, 8 + pos, mate), None),
        "X0": (copies(1, None, 8 + pos, across), leftc),
        "Z0": (copies(2, None, 4 + pos, me + 4), feeds),
        "D0x": (copies(3, 8 + pos_x, 8 + pos_x, mate), right),
        "D1": (copies(4, 4 + pos, 4 + pos, mate), has1),
        "X1": (copies(5, 4 + pos, 4 + pos, across), has1),
        "Z1": (copies(6, 4 + pos, pos, me + 4), has1 & feeds),
        "D1x": (copies(7, 4 + pos_x, 4 + pos_x, mate), has1),
        "D2": (copies(8, pos, pos, mate), has2),
        "X2": (copies(9, pos, pos, across), has2 & right),
        "D2x": (copies(10, pos_x, pos_x, mate), has2 & leftc),
    }

    def when(cond, fn):
        if cond is None:
            fn()
        else:
            pl.when(cond)(fn)

    def start(name):
        made, cond = moves[name]

        def go():
            for copy in made:
                copy.start()

        when(cond, go)

    def sent(name):
        made, cond = moves[name]

        def go():
            for copy in made:
                copy.wait_send()

        when(cond, go)

    def landed(slot, cond):
        def go():
            for w, buf in ((0, kbuf), (1, vbuf)):
                pltpu.make_async_copy(buf.at[slot], buf.at[slot], recv_sem.at[slot, w]).wait()

        when(cond, go)

    start("Z0")
    start("X0")
    start("D0")

    lane = lax.broadcasted_iota(jnp.int32, (8, 128), 1)
    firsts = jnp.full((8, 128), 2**30, jnp.int32)
    ends = jnp.full((8, 128), 2**30, jnp.int32)
    run = jnp.int32(0)
    for d in range(lens_ref.shape[0]):
        firsts = jnp.where(lane == d, run, firsts)
        run = run + lens_ref[d]
        ends = jnp.where(lane == d, run, ends)
    first_row, end_row = firsts[0:1], ends[0:1]

    def member(position):
        return (position >= first_row) & (position < end_row)

    base = me * rows

    @pl.loop(0, total_rows // TILE)
    def _(t):
        at = pl.ds(pl.multiple_of(t * TILE, TILE), TILE)
        token = (t * TILE + lax.broadcasted_iota(jnp.int32, (TILE, 128), 0)) // group
        qaug[at, 0:hdim] = q_ref[at, :]
        qaug[at, hdim:] = jnp.where(member(base + token), 1.0, 0.0).astype(jnp.bfloat16)

    @pl.loop(0, 12)
    def _(s):
        kpos = (me - pos - 8 + s) * rows + lax.broadcasted_iota(jnp.int32, (rows, 128), 0)
        kdoc[s] = jnp.where(member(kpos), 0.0, -BIG).astype(jnp.bfloat16)

    @pl.when(me < 8)
    def _():
        @pl.loop(0, 4)
        def _(s):
            kbuf[s] = jnp.zeros((rows, hdim), jnp.bfloat16)
            vbuf[s] = jnp.zeros((rows, hdim), jnp.bfloat16)

    scale = math.log2(math.e) / hdim**0.5
    ones = jnp.ones((rows, 128), jnp.bfloat16)

    def spread(x, width):
        return jnp.concatenate([x] * (width // 128), axis=1)

    def score(at, keys, docs):
        return lax.dot_general(
            qaug[at, :], jnp.concatenate([keys, docs], axis=1), (((1,), (1,)), ((), ())),
            preferred_element_type=jnp.float32) * scale

    @pl.loop(0, total_rows // TILE)
    def _(t):
        at = pl.ds(pl.multiple_of(t * TILE, TILE), TILE)
        s = score(at, k_ref[...], kdoc[8 + pos])
        token = (t * TILE + lax.broadcasted_iota(jnp.int32, (TILE, rows), 0)) // group
        s = jnp.where(lax.broadcasted_iota(jnp.int32, (TILE, rows), 1) <= token, s, -BIG)
        m = jnp.broadcast_to(jnp.max(s, axis=1, keepdims=True), (TILE, 128))
        p = jnp.exp2(s - spread(m, rows)).astype(jnp.bfloat16)
        top[at, :] = m
        acc[at, :] = jnp.dot(p, jnp.concatenate([v_ref[...], ones], axis=1),
                             preferred_element_type=jnp.float32)

    def both(at, a, b):
        keep = []
        sa = score(at, kbuf[a], kdoc[a])
        sb = score(at, kbuf[b], kdoc[b])
        m0 = top[at, :]
        m = jnp.maximum(m0, jnp.max(jnp.maximum(sa, sb), axis=1, keepdims=True))
        wide = spread(m, rows)
        pa = jnp.exp2(sa - wide).astype(jnp.bfloat16)
        pb = jnp.exp2(sb - wide).astype(jnp.bfloat16)
        top[at, :] = m
        grown = jnp.dot(pa, jnp.concatenate([vbuf[a], ones], axis=1), preferred_element_type=jnp.float32)
        grown = grown + jnp.dot(pb, jnp.concatenate([vbuf[b], ones], axis=1), preferred_element_type=jnp.float32)
        return acc[at, :] * spread(jnp.exp2(m0 - m), 256) + grown

    def pair(a, b, valid):
        @pl.when(valid)
        def _():
            @pl.loop(0, total_rows // TILE)
            def _(t):
                at = pl.ds(pl.multiple_of(t * TILE, TILE), TILE)
                acc[at, :] = both(at, a, b)

    def pick(if_right, if_left):
        return col * if_right + (1 - col) * if_left

    g1 = (4 + pos, 4 + pos_m)
    g2 = (4 + pos_x, 4 + pos_d)
    g3 = (pick(8 + pos_x, pos_x), pick(8 + pos_d, pos_d))
    g4 = (pos, core * (8 + pos_m) + (1 - core) * pos_m)

    landed(4 + pos, has1)
    start("Z1")
    start("X1")
    start("D1")
    landed(8 + pos_x, right)
    start("D0x")
    landed(8 + pos_m, None)
    landed(4 + pos_m, has1)
    landed(8 + pos_d, right)
    pair(pick(g3[0], g1[0]), pick(g3[1], g1[1]), right | has1)

    landed(pos, has2)
    start("X2")
    start("D2")
    landed(4 + pos_x, has1)
    start("D1x")
    landed(4 + pos_d, has1)
    pair(pick(g1[0], g2[0]), pick(g1[1], g2[1]), has1)

    landed(pos_m, has2)
    pair(pick(g2[0], g4[0]), pick(g2[1], g4[1]), (right & has1) | (leftc & (has2 | (core == 1))))

    landed(pos_x, has2 & leftc)
    start("D2x")
    landed(pos_d, has2 & leftc)
    last_a, last_b = pick(g4[0], g3[0]), pick(g4[1], g3[1])
    last_valid = has2 | (right & (core == 1))

    part = rows // heads
    tokens = TILE // group
    steps = part // tokens
    columns = pl.ds(pl.multiple_of(mine * (group * hdim), group * hdim), group * hdim)

    def finish(owner, t, own):
        at = pl.ds(pl.multiple_of(owner * (part * group) + t * TILE, TILE), TILE)

        @pl.when(last_valid)
        def _():
            whole = both(at, last_a, last_b)
            norm[...] = whole[:, 0:hdim] / whole[:, hdim:]

        @pl.when(jnp.logical_not(last_valid))
        def _():
            whole = acc[at, :]
            norm[...] = whole[:, 0:hdim] / whole[:, hdim:]

        local = pl.ds(pl.multiple_of(t * tokens, tokens), tokens)
        for g in range(group):
            piece = norm[pl.ds(g, tokens, stride=group), :].astype(jnp.bfloat16)
            if own is None:
                where = pl.ds(pl.multiple_of(mine * (group * hdim) + g * hdim, hdim), hdim)
                out_ref[local, where] = piece
            else:
                stage[own, local, g * hdim:(g + 1) * hdim] = piece

    def outgoing(d, t):
        local = pl.ds(pl.multiple_of(t * tokens, tokens), tokens)
        return pltpu.make_async_remote_copy(
            src_ref=stage.at[d - 1, local],
            dst_ref=out_ref.at[local, columns],
            send_sem=osend_sem.at[d - 1, t],
            recv_sem=orecv_sem.at[d - 1, t],
            device_id={"head": (mine + d) % heads},
            device_id_type=MESH,
        )

    for d in range(1, heads):
        @pl.loop(0, steps)
        def _(t):
            finish((mine + d) % heads, t, d - 1)
            outgoing(d, t).start()

    @pl.loop(0, steps)
    def _(t):
        finish(mine, t, None)

    for d in range(1, heads):
        @pl.loop(0, steps)
        def _(t):
            outgoing(d, t).wait_send()
            source = (mine + heads - d) % heads
            local = pl.ds(pl.multiple_of(t * tokens, tokens), tokens)
            cols = pl.ds(pl.multiple_of(source * (group * hdim), group * hdim), group * hdim)
            got = out_ref.at[local, cols]
            pltpu.make_async_copy(got, got, orecv_sem.at[d - 1, t]).wait()

    for name in moves:
        sent(name)


def on_device(mesh, queries, keys, values, doc_lengths):
    rows, group, hdim = queries.shape
    heads = mesh.shape["head"]
    n = mesh.shape["ctx"]
    bf16, f32 = jnp.bfloat16, jnp.float32
    part = rows // heads
    steps = part * group // TILE
    vmem = pl.BlockSpec(memory_space=pltpu.VMEM)
    return pl.pallas_call(
        functools.partial(kernel, n, heads),
        out_shape=jax.ShapeDtypeStruct((part, heads * group * hdim), bf16),
        in_specs=[pl.BlockSpec(memory_space=pltpu.SMEM), vmem, vmem, vmem],
        out_specs=vmem,
        scratch_shapes=[
            pltpu.VMEM((12, rows, hdim), bf16),
            pltpu.VMEM((12, rows, hdim), bf16),
            pltpu.VMEM((12, rows, 128), bf16),
            pltpu.VMEM((rows * group, hdim + 128), bf16),
            pltpu.VMEM((rows * group, hdim + 128), f32),
            pltpu.VMEM((rows * group, 128), f32),
            pltpu.VMEM((TILE, hdim), f32),
            pltpu.VMEM((heads - 1, part, group * hdim), bf16),
            pltpu.SemaphoreType.DMA((11, 2)),
            pltpu.SemaphoreType.DMA((12, 2)),
            pltpu.SemaphoreType.DMA((heads - 1, steps)),
            pltpu.SemaphoreType.DMA((heads - 1, steps)),
        ],
        compiler_params=pltpu.CompilerParams(
            collective_id=0, has_side_effects=True, vmem_limit_bytes=56 * 1024 * 1024),
    )(doc_lengths, queries.reshape(rows * group, hdim), keys.reshape(rows, hdim), values.reshape(rows, hdim))


def solution(mesh):
    placed = (P("ctx", "head", None), P("ctx", "head", None), P("ctx", "head", None), P())
    return jax.shard_map(
        functools.partial(on_device, mesh), mesh=mesh, in_specs=placed,
        out_specs=P(("ctx", "head"), None), check_vma=False
    )
```

profile of v0, /device:TPU:17, one launch (start us, length us, event | category | flops | bytes accessed | tf_op | source)
XLA Modules:
  0.0 68.6 jit_solution(2276375511149428759)
XLA Ops:
  0.0 66.3 %shard_map.46 = bf16[256,2048]{1,0:T(8,128)(2,1)} custom-call(s32[32]{0:T(128)} %lens_ref.1, bf16[4096,128]{1,0:T(8,128)(2,1)} %bitcast.3, bf16[512,128]{1,0:T(8,128)(2,1)} %bitcast.4, bf16[512,128]{1,0:T(8,128)(2,1)} %bitcast.5), custom_call_target="tpu_custom_call" | custom-call | tf_op jit(solution)/shard_map/pallas_call | solution.py:301
  66.3 2.3 %copy.6 = bf16[256,2048]{1,0:T(8,128)(2,1)} copy(bf16[256,2048]{1,0:T(8,128)(2,1)} %shard_map.46) | data formatting | bytes 2097152
where the time goes:
time: 68.8 us; the launch traced here: 68.6 us
  Pallas kernels  66.3 us (96%)
  local copies, waits for them, and re-layouts  2.3 us (3%)
    pallas_call x1, Pallas kernels, on_device(): pl.pallas_call(functools.partial(kernel, n, heads), out_shape=jax.ShapeDt...  66.3 us
    unnamed x1, local copies, waits for them, and re-layouts  2.3 us

commit v1 on v0

--- a/solution.py
+++ b/solution.py
@@ -10,10 +10,10 @@
 
 MESH = pl.DeviceIdType.MESH
 BIG = 1e30
-TILE = 512
-
-
-def kernel(n, heads, lens_ref, q_ref, k_ref, v_ref, out_ref,
+MOST = 1024
+
+
+def kernel(n, heads, tile, lens_ref, q_ref, k_ref, v_ref, out_ref,
            kbuf, vbuf, kdoc, qaug, acc, top, norm, stage,
            send_sem, recv_sem, osend_sem, orecv_sem):
     rows, hdim = k_ref.shape
@@ -128,10 +128,10 @@
 
     base = me * rows
 
-    @pl.loop(0, total_rows // TILE)
+    @pl.loop(0, total_rows // tile)
     def _(t):
-        at = pl.ds(pl.multiple_of(t * TILE, TILE), TILE)
-        token = (t * TILE + lax.broadcasted_iota(jnp.int32, (TILE, 128), 0)) // group
+        at = pl.ds(pl.multiple_of(t * tile, tile), tile)
+        token = (t * tile + lax.broadcasted_iota(jnp.int32, (tile, 128), 0)) // group
         qaug[at, 0:hdim] = q_ref[at, :]
         qaug[at, hdim:] = jnp.where(member(base + token), 1.0, 0.0).astype(jnp.bfloat16)
 
@@ -148,7 +148,6 @@
             vbuf[s] = jnp.zeros((rows, hdim), jnp.bfloat16)
 
     scale = math.log2(math.e) / hdim**0.5
-    ones = jnp.ones((rows, 128), jnp.bfloat16)
 
     def spread(x, width):
         return jnp.concatenate([x] * (width // 128), axis=1)
@@ -158,38 +157,41 @@
             qaug[at, :], jnp.concatenate([keys, docs], axis=1), (((1,), (1,)), ((), ())),
             preferred_element_type=jnp.float32) * scale
 
-    @pl.loop(0, total_rows // TILE)
+    @pl.loop(0, total_rows // tile)
     def _(t):
-        at = pl.ds(pl.multiple_of(t * TILE, TILE), TILE)
+        at = pl.ds(pl.multiple_of(t * tile, tile), tile)
         s = score(at, k_ref[...], kdoc[8 + pos])
-        token = (t * TILE + lax.broadcasted_iota(jnp.int32, (TILE, rows), 0)) // group
-        s = jnp.where(lax.broadcasted_iota(jnp.int32, (TILE, rows), 1) <= token, s, -BIG)
-        m = jnp.broadcast_to(jnp.max(s, axis=1, keepdims=True), (TILE, 128))
-        p = jnp.exp2(s - spread(m, rows)).astype(jnp.bfloat16)
+        token = (t * tile + lax.broadcasted_iota(jnp.int32, (tile, rows), 0)) // group
+        s = jnp.where(lax.broadcasted_iota(jnp.int32, (tile, rows), 1) <= token, s, -BIG)
+        m = jnp.broadcast_to(jnp.max(s, axis=1, keepdims=True), (tile, 128))
+        e = jnp.exp2(s - spread(m, rows))
         top[at, :] = m
-        acc[at, :] = jnp.dot(p, jnp.concatenate([v_ref[...], ones], axis=1),
-                             preferred_element_type=jnp.float32)
+        acc[at, 0:128] = jnp.dot(e.astype(jnp.bfloat16), v_ref[...], preferred_element_type=jnp.float32)
+        acc[at, 128:] = sum(e[:, k * 128:(k + 1) * 128] for k in range(rows // 128))
 
     def both(at, a, b):
-        keep = []
         sa = score(at, kbuf[a], kdoc[a])
         sb = score(at, kbuf[b], kdoc[b])
         m0 = top[at, :]
         m = jnp.maximum(m0, jnp.max(jnp.maximum(sa, sb), axis=1, keepdims=True))
         wide = spread(m, rows)
-        pa = jnp.exp2(sa - wide).astype(jnp.bfloat16)
-        pb = jnp.exp2(sb - wide).astype(jnp.bfloat16)
+        ea = jnp.exp2(sa - wide)
+        eb = jnp.exp2(sb - wide)
+        pa = ea.astype(jnp.bfloat16)
+        pb = eb.astype(jnp.bfloat16)
         top[at, :] = m
-        grown = jnp.dot(pa, jnp.concatenate([vbuf[a], ones], axis=1), preferred_element_type=jnp.float32)
-        grown = grown + jnp.dot(pb, jnp.concatenate([vbuf[b], ones], axis=1), preferred_element_type=jnp.float32)
-        return acc[at, :] * spread(jnp.exp2(m0 - m), 256) + grown
+        grown = jnp.dot(pa, vbuf[a], preferred_element_type=jnp.float32)
+        grown = grown + jnp.dot(pb, vbuf[b], preferred_element_type=jnp.float32)
+        factor = jnp.exp2(m0 - m)
+        tot = sum(ea[:, k * 128:(k + 1) * 128] + eb[:, k * 128:(k + 1) * 128] for k in range(rows // 128))
+        return jnp.concatenate([acc[at, 0:128] * factor + grown, acc[at, 128:] * factor + tot], axis=1)
 
     def pair(a, b, valid):
         @pl.when(valid)
         def _():
-            @pl.loop(0, total_rows // TILE)
+            @pl.loop(0, total_rows // tile)
             def _(t):
-                at = pl.ds(pl.multiple_of(t * TILE, TILE), TILE)
+                at = pl.ds(pl.multiple_of(t * tile, tile), tile)
                 acc[at, :] = both(at, a, b)
 
     def pick(if_right, if_left):
@@ -229,22 +231,22 @@
     last_valid = has2 | (right & (core == 1))
 
     part = rows // heads
-    tokens = TILE // group
+    tokens = tile // group
     steps = part // tokens
     columns = pl.ds(pl.multiple_of(mine * (group * hdim), group * hdim), group * hdim)
 
     def finish(owner, t, own):
-        at = pl.ds(pl.multiple_of(owner * (part * group) + t * TILE, TILE), TILE)
+        at = pl.ds(pl.multiple_of(owner * (part * group) + t * tile, tile), tile)
 
         @pl.when(last_valid)
         def _():
             whole = both(at, last_a, last_b)
-            norm[...] = whole[:, 0:hdim] / whole[:, hdim:]
+            norm[...] = whole[:, 0:hdim] / jnp.sum(whole[:, hdim:], axis=1, keepdims=True)
 
         @pl.when(jnp.logical_not(last_valid))
         def _():
             whole = acc[at, :]
-            norm[...] = whole[:, 0:hdim] / whole[:, hdim:]
+            norm[...] = whole[:, 0:hdim] / jnp.sum(whole[:, hdim:], axis=1, keepdims=True)
 
         local = pl.ds(pl.multiple_of(t * tokens, tokens), tokens)
         for g in range(group):
@@ -296,10 +298,11 @@
     n = mesh.shape["ctx"]
     bf16, f32 = jnp.bfloat16, jnp.float32
     part = rows // heads
-    steps = part * group // TILE
+    tile = min(MOST, part * group)
+    steps = part * group // tile
     vmem = pl.BlockSpec(memory_space=pltpu.VMEM)
     return pl.pallas_call(
-        functools.partial(kernel, n, heads),
+        functools.partial(kernel, n, heads, tile),
         out_shape=jax.ShapeDtypeStruct((part, heads * group * hdim), bf16),
         in_specs=[pl.BlockSpec(memory_space=pltpu.SMEM), vmem, vmem, vmem],
         out_specs=vmem,
@@ -310,7 +313,7 @@
             pltpu.VMEM((rows * group, hdim + 128), bf16),
             pltpu.VMEM((rows * group, hdim + 128), f32),
             pltpu.VMEM((rows * group, 128), f32),
-            pltpu.VMEM((TILE, hdim), f32),
+            pltpu.VMEM((tile, hdim), f32),
             pltpu.VMEM((heads - 1, part, group * hdim), bf16),
             pltpu.SemaphoreType.DMA((11, 2)),
             pltpu.SemaphoreType.DMA((12, 2)),

time: 68.8 us -> 55.8 us (0.81)
  Pallas kernels: 66.3 us -> 53.3 us
    pallas_call x1, Pallas kernels: 66.3 us -> 53.3 us  [on_device(): pl.pallas_call(functools.partial(kernel, n, heads, tile), out_shape=jax.S...]
where the time goes in v1:
time: 55.8 us; the launch traced here: 55.7 us
  Pallas kernels  53.3 us (96%)
  local copies, waits for them, and re-layouts  2.3 us (4%)
    pallas_call x1, Pallas kernels, on_device(): pl.pallas_call(functools.partial(kernel, n, heads, tile), out_shape=jax.S...  53.3 us
    unnamed x1, local copies, waits for them, and re-layouts  2.3 us

profile of v1, /device:TPU:17, one launch (start us, length us, event | category | flops | bytes accessed | tf_op | source)
XLA Modules:
  0.0 55.7 jit_solution(3998801561355081320)
XLA Ops:
  0.0 53.3 %shard_map.46 = bf16[256,2048]{1,0:T(8,128)(2,1)} custom-call(s32[32]{0:T(128)} %lens_ref.1, bf16[4096,128]{1,0:T(8,128)(2,1)} %bitcast.3, bf16[512,128]{1,0:T(8,128)(2,1)} %bitcast.4, bf16[512,128]{1,0:T(8,128)(2,1)} %bitcast.5), custom_call_target="tpu_custom_call" | custom-call | tf_op jit(solution)/shard_map/pallas_call | solution.py:304
  53.4 2.3 %copy.6 = bf16[256,2048]{1,0:T(8,128)(2,1)} copy(bf16[256,2048]{1,0:T(8,128)(2,1)} %shard_map.46) | data formatting | bytes 2097152
